TPU v7x, 512 devices: a 8x2x16 block of a 8x8x16 slice. The times are simulated.
512 devices in a mesh: groups: 2 (over y), ep: 128 (over z, x), hp: 2 (over core).
Axes of the slice: x: 8, y: 2, z: 16, core: 2. Of those that a mesh axis runs over, the one named last changes fastest.
The devices are a block of a 8x8x16 slice.
Arguments:
- x_pre: bfloat16 [14336, 1536], P(('groups', 'ep')), parts along dimension 0, may hold values from -6 to 6
- x_dec: bfloat16 [2048, 1536], P(('groups', 'ep')), parts along dimension 0, may hold values from -6 to 6
- prefill_query_rows: bfloat16 [14336, 2048], P(('groups', 'ep'), 'hp'), parts along dimension 0, may hold values from -240 to 240
- prefill_key_values: bfloat16 [2, 14336, 256], P(None, ('groups', 'ep'), 'hp'), parts along dimension 1, may hold values from -6.1 to 6.1
- decode_query_rows: bfloat16 [2048, 2048], P(('groups', 'ep'), 'hp'), parts along dimension 0, may hold values from -240 to 240
- decode_key_values: bfloat16 [2, 2048, 256], P(None, ('groups', 'ep'), 'hp'), parts along dimension 1, may hold values from -6 to 6
- cache: bfloat16 [2, 2048, 128, 256], P(None, ('groups', 'ep'), None, 'hp'), parts along dimension 1, may hold values from -6.1 to 6.1
- cache_len: int32 [2048], P(('groups', 'ep')), parts along dimension 0, may hold values from 2 to 128
- sinks: float32 [32], P('hp'), may hold values from -1 to 5
- o_weight: bfloat16 [2048, 1536], P('hp', 'ep'), may hold values from -0.125 to 0.125
- norm_gain: float32 [1536], replicated, may hold values from 0.5 to 1.5
- expert_ids: int32 [16384, 4], P(('groups', 'ep')), parts along dimension 0, may hold values from 0 to 63, all different within a row; in each aligned block of 64 rows (0 to 63, 64 to 127, ...) at most 6 rows name the same one
- route_logits: float32 [16384, 4], P(('groups', 'ep')), parts along dimension 0, may hold values from -6 to 6
- w_gate_up: bfloat16 [128, 2, 1536, 768], P('ep', None, None, 'hp'), may hold values from -0.15625 to 0.15625
- w_down: bfloat16 [128, 768, 1536], P('ep', 'hp'), may hold values from -0.15625 to 0.15625
Outputs:
- layer_out: bfloat16 [16384, 1536], P(('groups', 'ep', 'hp')), parts along dimension 0
There are 2 independent parts, one for each index of `groups`. A program takes and returns all parts, laid end to end along the dimension named above; an argument that names none is the same for every part. Nothing has to cross between parts.
Inputs may be any that keep to these rules, and one draw needn't show every extreme that they name: `expert_ids`: each row names 4 different experts; among the rows of one index of ep no expert is named by more than 6 rows, and in every draw some expert is named by exactly 6 rows of some index.
All inputs are finite; a program needn't handle non-finite values.
Results may differ from a plain program's by a relative error of at most 0.0065.
Values may be sent and summed in bfloat16 or wider, within the bound.
A program may use at most 64 MiB of HBM per device.

v0:
```python
import jax
import jax.numpy as jnp
from jax import lax
from jax.sharding import Mesh
from jax.sharding import PartitionSpec as P

HEAD_SIZE = 64
EP = ("ep_0", "ep_1")
GROUPS_EP = ("groups", "ep_0", "ep_1")
GROUPS_EP_HP = ("groups", "ep_0", "ep_1", "hp")


EPS = 1e-05


def laid_out(tiles, dim):
    tiles = jnp.moveaxis(tiles, 0, dim)
    shape = tiles.shape
    return tiles.reshape(*shape[:dim], shape[dim] * shape[dim + 1], *shape[dim + 2 :])


def all_blocks(shard, axes, order):
    tiles = shard[None]
    for k in order:
        tiles = lax.all_gather(tiles, axes[k], axis=0, tiled=True)
    current = [lax.axis_size(axes[k]) for k in reversed(order)]
    tiles = tiles.reshape(*current, *shard.shape)
    turned = sorted(range(len(order)), key=lambda place: order[len(order) - 1 - place])
    return tiles.transpose(*turned, *range(len(order), tiles.ndim)).reshape(-1, *shard.shape)


def gather_axes(shard, axes, order, dim):
    return laid_out(all_blocks(shard, axes, order), dim)


def copy_for_each(shard, axis):
    size = lax.axis_size(axis)
    return lax.all_to_all(
        jnp.broadcast_to(shard[None], (size, *shard.shape)), axis, 0, 0, tiled=True
    )


def of_everyone(shard, axis):
    everything = copy_for_each(shard, axis)
    return jnp.sum(everything, axis=0)


def gathered_copies(shard, axis, dim):
    tiles = copy_for_each(shard, axis)
    return laid_out(tiles, dim)


def split_up(shard, dim, size):
    shape = shard.shape
    tiles = shard.reshape(*shape[:dim], size, shape[dim] // size, *shape[dim + 1 :])
    return jnp.moveaxis(tiles, dim, 0)


def sum_at_owner(shard, axis, dim):
    tiles = split_up(shard, dim, lax.axis_size(axis))
    arrived = lax.all_to_all(tiles, axis, split_axis=0, concat_axis=0, tiled=True)
    return arrived.astype(jnp.float32).sum(axis=0)


def softmax_probability(scores, sink_logit_bias):
    top = jnp.maximum(jnp.max(scores, axis=-1, keepdims=True), sink_logit_bias)
    expo = jnp.exp(scores - top)
    total = jnp.sum(expo, axis=-1, keepdims=True) + jnp.exp(sink_logit_bias - top)
    return (expo / total).astype(jnp.bfloat16)


def rms_norm(stream, gain):
    mean_sq = jnp.mean(stream * stream, axis=-1, keepdims=True)
    return (stream * lax.rsqrt(mean_sq + EPS) * gain).astype(jnp.bfloat16)


def on_device(
    x_pre,
    x_dec,
    prefill_query_rows,
    prefill_key_values,
    decode_query_rows,
    decode_key_values,
    cache,
    cache_len,
    sinks,
    o_weight,
    norm_gain,
    expert_ids,
    route_logits,
    w_gate_up,
    w_down,
):
    pre_rows, width = x_pre.shape
    dec_rows = x_dec.shape[0]
    kv_heads = prefill_key_values.shape[2] // HEAD_SIZE
    q_heads = sinks.shape[0]
    head_group = q_heads // kv_heads
    kv_max = cache.shape[2]
    scale = HEAD_SIZE ** (-0.5)
    sink_logit_bias = sinks.reshape(kv_heads, head_group)[None, :, :, None]
    keys_here = prefill_key_values[0].reshape(pre_rows, kv_heads, HEAD_SIZE)
    values_here = prefill_key_values[1].reshape(pre_rows, kv_heads, HEAD_SIZE)
    query_rows = prefill_query_rows.reshape(pre_rows, kv_heads, head_group, HEAD_SIZE)
    scores = (
        jnp.einsum("qhgd,khd->qhgk", query_rows, keys_here, preferred_element_type=jnp.float32)
        * scale
    )
    places = jnp.arange(pre_rows, dtype=jnp.int32)
    visible = places[None, :] <= places[:, None]
    scores = jnp.where(visible[:, None, None, :], scores, -jnp.inf)
    weight_matrix = softmax_probability(scores, sink_logit_bias)
    pre_out = jnp.einsum(
        "qhgk,khd->qhgd", weight_matrix, values_here, preferred_element_type=jnp.float32
    )
    pre_out = pre_out.astype(jnp.bfloat16).reshape(pre_rows, q_heads * HEAD_SIZE)
    dec_queries = decode_query_rows.reshape(dec_rows, kv_heads, head_group, HEAD_SIZE)
    cached_key_rows = cache[0].reshape(dec_rows, kv_max, kv_heads, HEAD_SIZE)
    cached_value_rows = cache[1].reshape(dec_rows, kv_max, kv_heads, HEAD_SIZE)
    own_key_rows = decode_key_values[0].reshape(dec_rows, kv_heads, HEAD_SIZE)
    own_value_rows = decode_key_values[1].reshape(dec_rows, kv_heads, HEAD_SIZE)
    past_positions = (
        jnp.einsum(
            "shgd,sjhd->shgj", dec_queries, cached_key_rows, preferred_element_type=jnp.float32
        )
        * scale
    )
    live = jnp.arange(kv_max, dtype=jnp.int32)[None, :] < cache_len[:, None]
    past_positions = jnp.where(live[:, None, None, :], past_positions, -jnp.inf)
    own_token = (
        jnp.einsum("shgd,shd->shg", dec_queries, own_key_rows, preferred_element_type=jnp.float32)[
            ..., None
        ]
        * scale
    )
    dec_weights = softmax_probability(
        jnp.concatenate([past_positions, own_token], axis=-1), sink_logit_bias
    )
    dec_out = jnp.einsum(
        "shgj,sjhd->shgd",
        dec_weights[..., :kv_max],
        cached_value_rows,
        preferred_element_type=jnp.float32,
    )
    dec_out = (
        dec_out
        + dec_weights[..., kv_max:].astype(jnp.float32)
        * own_value_rows.astype(jnp.float32)[:, :, None, :]
    )
    dec_out = dec_out.astype(jnp.bfloat16).reshape(dec_rows, q_heads * HEAD_SIZE)
    attn_rows = jnp.concatenate([pre_out, dec_out], axis=0)
    resid = jnp.concatenate([x_pre, x_dec], axis=0).astype(jnp.float32)
    half = attn_rows.shape[0] // 2
    mine = lax.axis_index("hp") * half
    head_part = jnp.dot(
        attn_rows, gather_axes(o_weight, EP, (0, 1), 1), preferred_element_type=jnp.float32
    )
    summed = of_everyone(head_part, "hp")
    whole = resid + summed
    normed = rms_norm(whole, norm_gain)
    stream = lax.dynamic_slice_in_dim(whole, mine, half, 0)
    tokens_here, topk = expert_ids.shape
    holders = lax.axis_size(EP)
    experts = holders // 2
    slot = min(
        tokens_here, 2 * ((3 * max(1, (tokens_here * topk + experts - 1) // experts) + 3) // 4)
    )
    plane = slot // 2
    flat_ids = expert_ids.reshape(-1)
    onehot = (flat_ids[:, None] == jnp.arange(experts, dtype=jnp.int32)[None, :]).astype(jnp.int32)
    rank = jnp.sum(jnp.cumsum(onehot, axis=0) * onehot, axis=1) - 1
    position = (flat_ids * slot + rank).reshape(tokens_here, topk)
    columns = jnp.arange(experts * slot, dtype=jnp.int32)[None, None, :] == position[:, :, None]
    picked_rows = jnp.any(columns, axis=1).T.astype(jnp.bfloat16)
    per_expert = (
        jnp.dot(picked_rows, normed, preferred_element_type=jnp.float32)
        .astype(jnp.bfloat16)
        .reshape(experts, slot, width)
    )
    send = jnp.repeat(per_expert, 2, axis=0)
    own_plane = lax.dynamic_slice_in_dim(send, lax.axis_index("hp") * plane, plane, 1)
    arrived_plane = lax.all_to_all(own_plane, EP, split_axis=0, concat_axis=0, tiled=True)
    arrived = gathered_copies(arrived_plane, "hp", 1)
    rows = arrived.reshape(-1, width)
    gate = jnp.dot(rows, w_gate_up[0, 0], preferred_element_type=jnp.float32)
    upper = jnp.dot(rows, w_gate_up[0, 1], preferred_element_type=jnp.float32)
    hidden = ((upper + 1.0) * gate * jax.nn.sigmoid(1.702 * gate)).astype(jnp.bfloat16)
    partial_out = jnp.dot(hidden, w_down[0], preferred_element_type=jnp.float32).reshape(
        -1, slot, width
    )
    share = sum_at_owner(partial_out.astype(jnp.bfloat16), "hp", 1).astype(jnp.bfloat16)
    returned = lax.all_to_all(share, EP, split_axis=0, concat_axis=0, tiled=True)
    mix = jax.nn.softmax(route_logits, axis=-1)
    blend = jnp.sum(jnp.where(columns, mix[:, :, None], 0.0), axis=1).reshape(
        tokens_here, experts, slot
    )
    blend = jnp.repeat(blend, 2, axis=1)
    blend_plane = lax.dynamic_slice_in_dim(blend, lax.axis_index("hp") * plane, plane, 2).reshape(
        tokens_here, holders * plane
    )
    terms = jnp.dot(
        blend_plane,
        returned.reshape(-1, width).astype(jnp.float32),
        precision=lax.Precision.HIGHEST,
    )
    moe = sum_at_owner(terms.astype(jnp.bfloat16), "hp", 0)
    return (stream + moe).astype(jnp.bfloat16)


def solution(mesh):
    torus = Mesh(
        mesh.devices.reshape(mesh.shape["groups"], 16, 8, mesh.shape["hp"]),
        ("groups", "ep_0", "ep_1", "hp"),
    )
    return jax.shard_map(
        on_device,
        mesh=torus,
        in_specs=(
            P(GROUPS_EP, None),
            P(GROUPS_EP, None),
            P(GROUPS_EP, "hp"),
            P(None, GROUPS_EP, "hp"),
            P(GROUPS_EP, "hp"),
            P(None, GROUPS_EP, "hp"),
            P(None, GROUPS_EP, None, "hp"),
            P(GROUPS_EP),
            P("hp"),
            P("hp", EP),
            P(),
            P(GROUPS_EP, None),
            P(GROUPS_EP, None),
            P(EP, None, None, "hp"),
            P(EP, "hp", None),
        ),
        out_specs=P(GROUPS_EP_HP, None),
        check_vma=False,
    )
```

profile of v0, /device:TPU:65, one launch (start us, length us, event | category | flops | bytes accessed | tf_op | source)
XLA Modules:
  0.0 380.8 jit_solution(8513952955429587322)
XLA Ops:
  6.6 65.3 %all-gather = bf16[16384,12]{0,1:T(8,128)(2,1)S(1)} all-gather(bf16[1024,12]{0,1:T(8,128)(2,1)} %param.24), channel_id=2, replica_groups=mesh['groups'=2,'ep_0'=16,'ep_1'=8,'hp'=2] {'ep_0'}, dimensions={0}, use_global_device_ids=true | all-gather | bytes 417792 | tf_op jit(solution)/shard_map/all_gather | solution.py:25
  72.2 0.8 slice_bitcast_fusion
  73.4 0.6 reduce-window.6
  76.0 0.7 copy.190
  77.2 0.3 fusion.15
  78.2 0.4 fusion.41
  79.5 44.3 %all-gather.3.cloned.1.call-done = bf16[128,1024,12]{1,0,2:T(8,128)(2,1)} async-done(((bf16[16,1024,12]{1,0,2:T(8,128)(2,1)}), bf16[128,1024,12]{1,0,2:T(8,128)(2,1)}) %all-gather.3.cloned.1.call-update) | async-done | bytes 3145744 | tf_op jit(solution)/shard_map/all_gather | solution.py:25
  123.8 3.9 %copy.245 = bf16[16,8,1024,12]{2,1,0,3:T(8,128)(2,1)S(1)} copy(bf16[16,8,1024,12]{2,0,1,3:T(8,128)(2,1)} %bitcast.89) | data formatting | bytes 6291456 | tf_op jit(solution)/shard_map/transpose | solution.py:29
  127.6 3.7 copy.197
  131.4 6.2 %reshape.166 = bf16[1024,1536]{0,1:T(8,128)(2,1)} reshape(bf16[1024,128,12]{0,2,1:T(8,128)(2,1)} %copy.197) | data formatting | bytes 6291456 | tf_op jit(solution)/shard_map/reshape | solution.py:19
  137.5 3.0 fusion.24
  140.6 5.9 %all_to_all.30 = f32[2,64,1536]{2,1,0:T(8,128)S(1)} all-to-all(f32[2,64,1536]{2,1,0:T(8,128)S(1)} %broadcast_in_dim.47), channel_id=1, replica_groups=mesh['groups'=2,'ep_0'=16,'ep_1'=8,'hp'=2] {'hp'}, dimensions={0} | all-to-all | bytes 1572864 | tf_op jit(solution)/shard_map/all_to_all | solution.py:38
  146.7 0.7 copy-done.1
  147.5 1.6 convolution_convert_fusion.1
  149.0 2.2 reshape.170
  151.5 0.8 constant_dynamic-slice_fusion
  152.3 90.6 %all_to_all.31 = bf16[128,3,1536]{2,1,0:T(4,128)(2,1)S(1)} all-to-all(bf16[128,3,1536]{2,1,0:T(4,128)(2,1)S(1)} %constant_dynamic-slice_fusion), channel_id=1, replica_groups=mesh['groups'=2,'ep_0'=16,'ep_1'=8,'hp'=2] {'ep_0','ep_1'}, dimensions={0} | all-to-all | bytes 2359296 | tf_op jit(solution)/shard_map/all_to_all | solution.py:182
  243.3 10.1 %all_to_all.32 = bf16[2,128,3,1536]{3,1,2,0:T(8,128)(2,1)S(1)} all-to-all(bf16[2,128,3,1536]{3,1,2,0:T(8,128)(2,1)S(1)} %broadcast_in_dim.86), channel_id=1, replica_groups=mesh['groups'=2,'ep_0'=16,'ep_1'=8,'hp'=2] {'hp'}, dimensions={0} | all-to-all | bytes 4718592 | tf_op jit(solution)/shard_map/all_to_all | solution.py:38
  253.4 3.7 copy.206
  257.1 5.3 %reshape_reshape.3 = bf16[768,1536]{1,0:T(8,128)(2,1)S(1)} reshape(bf16[128,2,3,1536]{3,2,1,0:T(4,128)(2,1)} %copy.206) | data formatting | bytes 4718592 | tf_op jit(solution)/shard_map/reshape;reshape | solution.py:184
  262.5 2.8 fusion.7
  265.3 2.3 fusion.3
  267.6 1.3 dot_general.44
  268.9 1.4 convolution_convert_fusion
  270.3 5.7 %all_to_all.33 = bf16[2,128,3,1536]{3,1,2,0:T(8,128)(2,1)S(1)} all-to-all(bf16[2,128,3,1536]{3,1,2,0:T(8,128)(2,1)S(1)} %bitcast.90), channel_id=1, replica_groups=mesh['groups'=2,'ep_0'=16,'ep_1'=8,'hp'=2] {'hp'}, dimensions={0} | all-to-all | bytes 4718592 | tf_op jit(solution)/shard_map/all_to_all | solution.py:61
  276.0 1.8 reduce_sum.91
  277.7 3.4 copy.208
  281.2 12.9 %all-to-all-start.4 = ((bf16[128,3,1536]{2,1,0:T(4,128)(2,1)}), bf16[128,3,1536]{2,1,0:T(4,128)(2,1)S(1)}, u32[]{:S(2)}, u32[]{:S(2)}) async-start(bf16[128,3,1536]{2,1,0:T(4,128)(2,1)} %copy.208), calls=%async_computation.4 | async-start | bytes 3145728 | tf_op jit(solution)/shard_map/all_to_all | solution.py:192
  294.5 69.4 %all-to-all-done.4 = bf16[128,3,1536]{2,1,0:T(4,128)(2,1)S(1)} async-done(((bf16[128,3,1536]{2,1,0:T(4,128)(2,1)}), bf16[128,3,1536]{2,1,0:T(4,128)(2,1)S(1)}, u32[]{:S(2)}, u32[]{:S(2)}) %all-to-all-start.4) | async-done | bytes 1179680 | tf_op jit(solution)/shard_map/all_to_all | solution.py:192
  364.0 0.9 fusion
  364.9 8.4 %all_to_all.34 = bf16[2,32,1536]{2,1,0:T(8,128)(2,1)S(1)} all-to-all(bf16[2,32,1536]{2,1,0:T(8,128)(2,1)S(1)} %bitcast.95), channel_id=1, replica_groups=mesh['groups'=2,'ep_0'=16,'ep_1'=8,'hp'=2] {'hp'}, dimensions={0} | all-to-all | bytes 393216 | tf_op jit(solution)/shard_map/all_to_all | solution.py:61
  373.3 0.7 add_convert_fusion
  (96 shorter events, 6.1 us)
Async XLA Ops:
  6.5 262.4 %copy-start = (bf16[1,384,1536]{2,1,0:T(8,128)(2,1)S(1)}, bf16[1,384,1536]{2,1,0:T(8,128)(2,1)}, u32[]{:S(2)}) copy-start(bf16[1,384,1536]{2,1,0:T(8,128)(2,1)} %param.29) | copy-start | bytes 3538948
  6.6 66.5 %copy-start.11 = (s32[64,4]{0,1:T(4,128)S(1)}, s32[64,4]{0,1:T(4,128)}, u32[]{:S(2)}) copy-start(s32[64,4]{0,1:T(4,128)} %param.26) | copy-start | bytes 3076
  6.6 68.0 %copy-start.3 = (bf16[2,8,128,128]{3,2,1,0:T(8,128)(2,1)S(1)}, bf16[2,8,128,128]{3,2,1,0:T(8,128)(2,1)}, u32[]{:S(2)}) copy-start(bf16[2,8,128,128]{3,2,1,0:T(8,128)(2,1)} %param.21) | copy-start | bytes 1572868
  6.6 117.2 %all-gather.3.cloned.1.call-start = ((), (), s32[]{:S(2)}) async-start(), calls=%async_computation.6 | async-start | bytes 3538944 | tf_op jit(solution)/shard_map/all_gather | solution.py:25
  72.2 2.6 copy-start.9
  73.0 2.1 copy-start.12
  73.0 2.2 copy-start.14
  73.0 2.3 copy-start.15
  76.9 0.9 copy-start.5
  77.0 0.9 copy-start.6
  140.6 6.0 %copy-start.4 = (bf16[56,1536]{1,0:T(8,128)(2,1)S(1)}, bf16[56,1536]{1,0:T(8,128)(2,1)}, u32[]{:S(2)}) copy-start(bf16[56,1536]{1,0:T(8,128)(2,1)} %param.15) | copy-start | bytes 516100
  140.6 6.0 %copy-start.7 = (bf16[8,1536]{1,0:T(8,128)(2,1)S(1)}, bf16[8,1536]{1,0:T(8,128)(2,1)}, u32[]{:S(2)}) copy-start(bf16[8,1536]{1,0:T(8,128)(2,1)} %param.16) | copy-start | bytes 73732
  140.6 6.9 %copy-start.10 = (f32[1536]{0:T(1024)S(1)}, f32[1536]{0:T(1024)}, u32[]{:S(2)}) copy-start(f32[1536]{0:T(1024)} %param.25) | copy-start | bytes 18436
  146.7 0.7 copy-start.1
  262.5 2.8 copy-start.13
  281.2 12.9 %copy-start.8 = (f32[64,4]{0,1:T(4,128)S(1)}, f32[64,4]{0,1:T(4,128)}, u32[]{:S(2)}) copy-start(f32[64,4]{0,1:T(4,128)} %param.27) | copy-start | bytes 3076
  281.2 82.7 %all-to-all-start.4 = ((bf16[128,3,1536]{2,1,0:T(4,128)(2,1)}), bf16[128,3,1536]{2,1,0:T(4,128)(2,1)S(1)}, u32[]{:S(2)}, u32[]{:S(2)}) async-start(bf16[128,3,1536]{2,1,0:T(4,128)(2,1)} %copy.208), calls=%async_computation.4 | async-start | bytes 3145728 | tf_op jit(solution)/shard_map/all_to_all | solution.py:192
  294.5 78.8 %copy-start.2 = (f32[64,1536]{1,0:T(8,128)S(1)}, f32[64,1536]{1,0:T(8,128)}, u32[]{:S(2)}) copy-start(f32[64,1536]{1,0:T(8,128)} %copy-done.1) | copy-start | bytes 1179652
Sparse Core Ops, SparseCore 0:
  73.2 50.5 all-gather.2
where the time goes:
time: 382 us; the launch traced here: 381 us
  blocking collectives  186 us (49%)
  waiting for transfers between devices  114 us (30%)
  local copies, waits for them, and re-layouts  36.6 us (10%)
  between operations  13.9 us (4%)
  matrix products  13.3 us (3%)
  starting transfers between devices  12.9 us (3%)
  other arithmetic  4.5 us (1%)
    all_to_all x1, blocking collectives, on_device(): lax.all_to_all(own_plane, EP, split_axis=0, concat_axis=0, tiled=True)  90.6 us
    all_to_all x1, waiting for transfers between devices, on_device(): lax.all_to_all(share, EP, split_axis=0, concat_axis=0, tiled=True)  69.4 us
    all_gather x1, blocking collectives, all_blocks(): tiles = lax.all_gather(tiles, axes[k], axis=0, tiled=True)  65.3 us
    all_gather x1, waiting for transfers between devices, all_blocks(): tiles = lax.all_gather(tiles, axes[k], axis=0, tiled=True)  44.3 us
    all_to_all x2, blocking collectives, copy_for_each(): lax.all_to_all(jnp.broadcast_to(shard[None], (size, *shard.shape)), axis,...  16 us
    all_to_all x2, blocking collectives, sum_at_owner(): lax.all_to_all(tiles, axis, split_axis=0, concat_axis=0, tiled=True)  14 us
    all_to_all x1, starting transfers between devices, on_device(): lax.all_to_all(share, EP, split_axis=0, concat_axis=0, tiled=True)  12.9 us
  transfers between devices with their start and end apart: 2, of which 2 were waited for; matrix products, arithmetic and copies ran while one was open for 2% of the time, Pallas kernels for 0%

commit v1 on v0

v1 whole, which is shorter than its diff:
```python
import functools

import jax
import jax.numpy as jnp
import numpy as np
from jax import lax
from jax.experimental import pallas as pl
from jax.experimental.pallas import tpu as pltpu
from jax.sharding import Mesh
from jax.sharding import PartitionSpec as P

HEAD_SIZE = 64
EP = ("ep_0", "ep_1")
GROUPS_EP = ("groups", "ep_0", "ep_1")
GROUPS_EP_HP = ("groups", "ep_0", "ep_1", "hp")
EPS = 1e-05
MESH = pl.DeviceIdType.MESH
F32 = jnp.float32
BF16 = jnp.bfloat16


def softmax_probability(scores, sink_logit_bias):
    top = jnp.maximum(jnp.max(scores, axis=-1, keepdims=True), sink_logit_bias)
    expo = jnp.exp(scores - top)
    total = jnp.sum(expo, axis=-1, keepdims=True) + jnp.exp(sink_logit_bias - top)
    return (expo / total).astype(BF16)


def attention(
    prefill_query_rows,
    prefill_key_values,
    decode_query_rows,
    decode_key_values,
    cache,
    cache_len,
    sinks,
):
    pre_rows = prefill_query_rows.shape[0]
    dec_rows = decode_query_rows.shape[0]
    kv_heads = prefill_key_values.shape[2] // HEAD_SIZE
    q_heads = sinks.shape[0]
    head_group = q_heads // kv_heads
    kv_max = cache.shape[2]
    scale = HEAD_SIZE ** (-0.5)
    sink_logit_bias = sinks.reshape(kv_heads, head_group)[None, :, :, None]
    keys_here = prefill_key_values[0].reshape(pre_rows, kv_heads, HEAD_SIZE)
    values_here = prefill_key_values[1].reshape(pre_rows, kv_heads, HEAD_SIZE)
    query_rows = prefill_query_rows.reshape(pre_rows, kv_heads, head_group, HEAD_SIZE)
    scores = jnp.einsum("qhgd,khd->qhgk", query_rows, keys_here, preferred_element_type=F32) * scale
    places = jnp.arange(pre_rows, dtype=jnp.int32)
    visible = places[None, :] <= places[:, None]
    scores = jnp.where(visible[:, None, None, :], scores, -jnp.inf)
    weight_matrix = softmax_probability(scores, sink_logit_bias)
    pre_out = jnp.einsum("qhgk,khd->qhgd", weight_matrix, values_here, preferred_element_type=F32)
    pre_out = pre_out.astype(BF16).reshape(pre_rows, q_heads * HEAD_SIZE)
    dec_queries = decode_query_rows.reshape(dec_rows, kv_heads, head_group, HEAD_SIZE)
    cached_key_rows = cache[0].reshape(dec_rows, kv_max, kv_heads, HEAD_SIZE)
    cached_value_rows = cache[1].reshape(dec_rows, kv_max, kv_heads, HEAD_SIZE)
    own_key_rows = decode_key_values[0].reshape(dec_rows, kv_heads, HEAD_SIZE)
    own_value_rows = decode_key_values[1].reshape(dec_rows, kv_heads, HEAD_SIZE)
    past_positions = (
        jnp.einsum("shgd,sjhd->shgj", dec_queries, cached_key_rows, preferred_element_type=F32) * scale
    )
    live = jnp.arange(kv_max, dtype=jnp.int32)[None, :] < cache_len[:, None]
    past_positions = jnp.where(live[:, None, None, :], past_positions, -jnp.inf)
    own_token = (
        jnp.einsum("shgd,shd->shg", dec_queries, own_key_rows, preferred_element_type=F32)[..., None]
        * scale
    )
    dec_weights = softmax_probability(
        jnp.concatenate([past_positions, own_token], axis=-1), sink_logit_bias
    )
    dec_out = jnp.einsum(
        "shgj,sjhd->shgd", dec_weights[..., :kv_max], cached_value_rows, preferred_element_type=F32
    )
    dec_out = (
        dec_out
        + dec_weights[..., kv_max:].astype(F32) * own_value_rows.astype(F32)[:, :, None, :]
    )
    dec_out = dec_out.astype(BF16).reshape(dec_rows, q_heads * HEAD_SIZE)
    return jnp.concatenate([pre_out, dec_out], axis=0)


def remote(src, dst, send_sem, recv_sem, where):
    return pltpu.make_async_remote_copy(
        src_ref=src,
        dst_ref=dst,
        send_sem=send_sem,
        recv_sem=recv_sem,
        device_id=where,
        device_id_type=MESH,
    )


def greet(places):
    barrier = pltpu.get_barrier_semaphore()
    for place in places:
        pl.semaphore_signal(barrier, inc=1, device_id=place, device_id_type=MESH)
    pl.semaphore_wait(barrier, len(places))


def shifted(me, by, n):
    return lax.rem(me + (by + 2 * n), n)


def ring_gather(axis, n, me, view, subs, send_sems, recv_sems, sent):
    half = n // 2
    ways = ((0, -1, shifted(me, 1, n)), (1, 1, shifted(me, -1, n)))

    def used(step, way, sub):
        return step < half or sub % 2 == way

    def copy(step, way, sign, to, sub):
        block = view(shifted(me, sign * (step - 1), n), sub)
        at = (way * half + step - 1) * subs + sub
        return remote(block, block, send_sems.at[at], recv_sems.at[at], {axis: to})

    def arrival(step, way, sign, to, sub):
        block = view(shifted(me, sign * step, n), sub)
        at = (way * half + step - 1) * subs + sub
        return remote(block, block, send_sems.at[at], recv_sems.at[at], {axis: to})

    for sub in range(subs):
        for way, sign, to in ways:
            if used(1, way, sub):
                c = copy(1, way, sign, to, sub)
                c.start()
                sent.append(c)
    yield
    for step in range(1, half + 1):
        for sub in range(subs):
            for way, sign, to in ways:
                if not used(step, way, sub):
                    continue
                arrival(step, way, sign, to, sub).wait_recv()
                if step < half and used(step + 1, way, sub):
                    c = copy(step + 1, way, sign, to, sub)
                    c.start()
                    sent.append(c)
        yield


def ring_sems(n, subs):
    return pltpu.SemaphoreType.DMA((n * subs,))


def in_turn(*rings):
    rings = list(rings)
    while rings:
        for ring in list(rings):
            try:
                next(ring)
            except StopIteration:
                rings.remove(ring)


def nt(a, b):
    return lax.dot_general(a, b, (((1,), (1,)), ((), ())), preferred_element_type=F32)


def project_kernel(
    nz,
    nx,
    width_of,
    weight,
    attn,
    x_pre,
    x_dec,
    gain,
    info,
    pick_a,
    pick_b,
    stream,
    normed,
    info_all,
    small_a,
    small_b,
    big_a,
    big_b,
    sum_a,
    sum_b,
    from_core,
    squares,
    squares_in,
    small_a_send,
    small_a_recv,
    small_b_send,
    small_b_recv,
    big_a_send,
    big_a_recv,
    big_b_send,
    big_b_recv,
    info_send,
    info_recv,
    core_send,
    core_recv,
):
    z, x, h = lax.axis_index("ep_0"), lax.axis_index("ep_1"), lax.axis_index("hp")
    other = 1 - h
    greet(
        [
            {"ep_0": shifted(z, 1, nz)},
            {"ep_0": shifted(z, -1, nz)},
            {"ep_1": shifted(x, 1, nx)},
            {"ep_1": shifted(x, -1, nx)},
            {"hp": other},
        ]
    )
    k_half = weight.shape[1] // 2
    tokens = stream.shape[0]
    cols = stream.shape[1]
    small_a[x] = weight[:, 0:k_half]
    small_b[z] = weight[:, k_half : 2 * k_half]
    info_all[z] = info[...]
    sent = []
    ring_a = ring_gather(
        "ep_1", nx, x, lambda b, s: small_a.at[b], 1, small_a_send, small_a_recv, sent
    )
    ring_b = ring_gather(
        "ep_0", nz, z, lambda b, s: small_b.at[b], 1, small_b_send, small_b_recv, sent
    )
    next(ring_a)
    next(ring_b)
    for _ in range(nx // 2):
        next(ring_a)
    a_rows = big_a.shape[1]
    b_rows = big_b.shape[1]
    packed = jnp.dot(
        pick_a[...], small_a[...].reshape(-1, k_half), preferred_element_type=F32
    ).astype(BF16)
    big_a[z] = packed
    large_a = ring_gather(
        "ep_0",
        nz,
        z,
        lambda b, s: big_a.at[b, pl.ds(s * (a_rows // 2), a_rows // 2), :],
        2,
        big_a_send,
        big_a_recv,
        sent,
    )
    next(large_a)
    for _ in range(nz // 2):
        next(ring_b)
    packed = jnp.dot(
        pick_b[...], small_b[...].reshape(-1, k_half), preferred_element_type=F32
    ).astype(BF16)
    big_b[x] = packed
    large_b = ring_gather(
        "ep_1",
        nx,
        x,
        lambda b, s: big_b.at[b, pl.ds(s * (b_rows // 4), b_rows // 4), :],
        4,
        big_b_send,
        big_b_recv,
        sent,
    )
    next(large_b)
    tell = ring_gather("ep_0", nz, z, lambda b, s: info_all.at[b], 1, info_send, info_recv, sent)
    next(tell)
    for step in range(1, nz // 2 + 1):
        next(large_a)
        if step % (nz // nx) == 0:
            next(large_b)
        next(tell)
    attn_a = attn[:, 0:k_half]
    attn_b = attn[:, k_half : 2 * k_half]
    for b in range(nz):
        sum_a[b * a_rows : (b + 1) * a_rows, :] = nt(big_a[b], attn_a)
    for b in range(nx):
        sum_b[b * b_rows : (b + 1) * b_rows, :] = nt(big_b[b], attn_b)
    w = width_of
    for b in range(nz):
        for c in range(nx):
            at_a = (b * nx + c) * w
            at_b = (c * nz + b) * w
            sum_a[at_a : at_a + w, :] = sum_a[at_a : at_a + w, :] + sum_b[at_b : at_b + w, :]
    mine = pl.multiple_of(h * cols, cols)
    theirs = pl.multiple_of(other * cols, cols)
    swap = remote(
        sum_a.at[pl.ds(theirs, cols), :],
        from_core,
        core_send.at[0],
        core_recv.at[0],
        {"hp": other},
    )
    swap.start()
    swap.wait()
    summed = jnp.transpose(sum_a[pl.ds(mine, cols), :] + from_core[...])
    n_pre = x_pre.shape[0]
    stream[0:n_pre, :] = summed[0:n_pre] + x_pre[:, pl.ds(mine, cols)].astype(F32)
    stream[n_pre:tokens, :] = summed[n_pre:tokens] + x_dec[:, pl.ds(mine, cols)].astype(F32)
    value = stream[...]
    total = jnp.sum(value * value, axis=-1, keepdims=True)
    squares[...] = jnp.broadcast_to(total, squares.shape)
    swap = remote(squares, squares_in, core_send.at[1], core_recv.at[1], {"hp": other})
    swap.start()
    swap.wait()
    total = total + squares_in[:, 0:1]
    scale = lax.rsqrt(total / (2 * cols) + EPS)
    normed[...] = (value * scale * gain[:, pl.ds(mine, cols)]).astype(BF16)
    for c in sent:
        c.wait_send()


def places_around(nz, nx):
    z, x, h = lax.axis_index("ep_0"), lax.axis_index("ep_1"), lax.axis_index("hp")
    sign = 1 - 2 * lax.rem(x, 2)

    def near(by):
        return lax.rem(x + by * sign + 2 * nx, nx)

    return z, x, h, near


REACH = {1: -1, 2: 2, 3: -3}
ORDER = (3, 2, 1)


def friends(nz, z, h, near):
    return [
        {"ep_0": shifted(z, 1, nz)},
        {"ep_0": shifted(z, -1, nz)},
        {"hp": 1 - h},
        {"ep_1": near(1)},
        {"ep_1": near(-1)},
        {"ep_1": near(2)},
        {"ep_1": near(-2)},
        {"ep_1": near(-3)},
    ]


def dispatch_kernel(
    nz,
    nx,
    normed,
    info_all,
    rows,
    tok,
    onehot,
    picked,
    z_send,
    z_recv,
    direct_send,
    direct_recv,
    pair_send,
    pair_recv,
    core_send,
    core_recv,
):
    z, x, h, near = places_around(nz, nx)
    other = 1 - h
    greet(friends(nz, z, h, near))
    tokens, cols = normed.shape
    pairs, per_pair = picked.shape[0], picked.shape[1]
    tok[z] = normed[...]
    sent = []
    part = tokens // 2
    ring = ring_gather(
        "ep_0", nz, z, lambda b, s: tok.at[b, pl.ds(s * part, part), :], 2, z_send, z_recv, sent
    )
    next(ring)
    slots = pairs * per_pair
    first = (z * slots).astype(F32)
    target = lax.broadcasted_iota(jnp.int32, (slots, 128), 0).astype(F32) + first
    lower = lax.broadcasted_iota(jnp.int32, (8, 128), 1) < tokens
    for j in range(nz // 2):
        codes = jnp.where(lower, info_all[2 * j], info_all[2 * j + 1])
        hit = jnp.zeros((slots, 128), F32)
        for k in range(4):
            hit = jnp.where(codes[k : k + 1, :] == target, 1.0, hit)
        onehot[:, 128 * j : 128 * (j + 1)] = hit.astype(BF16)
    for _ in range(nz // 2):
        next(ring)
    everything = tok[...].reshape(nz * tokens, cols)
    for p in range(pairs):
        picked[p] = jnp.dot(
            onehot[p * per_pair : (p + 1) * per_pair, :], everything, preferred_element_type=F32
        ).astype(BF16)
    mine = x // 2
    piece = per_pair // 2

    def cut(ref, sub):
        return ref.at[pl.ds(sub * piece, piece), :]

    for sub in range(2):
        for k in ORDER:
            to = near(REACH[k])
            c = remote(
                cut(picked.at[to // 2], sub),
                cut(rows.at[h, x], sub),
                direct_send.at[2 * k + sub],
                direct_recv.at[2 * k + sub],
                {"ep_1": to},
            )
            c.start()
            sent.append(c)
        c = remote(
            cut(picked.at[mine], sub),
            cut(rows.at[h, x], sub),
            pair_send.at[sub],
            pair_recv.at[sub],
            {"ep_1": near(1)},
        )
        c.start()
        sent.append(c)
    rows[h, x] = picked[mine]
    crossing = []

    def cross(source, sub, at):
        block = cut(rows.at[h, source], sub)
        c = remote(
            block, block, core_send.at[2 * at + sub], core_recv.at[2 * at + sub], {"hp": other}
        )
        c.start()
        sent.append(c)
        there = cut(rows.at[other, source], sub)
        crossing.append(
            remote(
                there, there, core_send.at[2 * at + sub], core_recv.at[2 * at + sub], {"hp": other}
            )
        )

    cross(x, 0, 0)
    cross(x, 1, 0)
    for sub in range(2):
        for k in (1, 2, 3):
            source = near(-k)
            block = cut(rows.at[h, source], sub)
            at = 2 * k + sub
            remote(
                block, block, direct_send.at[at], direct_recv.at[at], {"ep_1": near(1)}
            ).wait_recv()
            c = remote(block, block, pair_send.at[at], pair_recv.at[at], {"ep_1": near(1)})
            c.start()
            sent.append(c)
            cross(source, sub, k)
    for sub in range(2):
        for k in range(4):
            source = near(1 + k)
            block = cut(rows.at[h, source], sub)
            at = 2 * k + sub
            remote(block, block, pair_send.at[at], pair_recv.at[at], {"ep_1": near(1)}).wait_recv()
            cross(source, sub, 4 + k)
    for c in crossing:
        c.wait_recv()
    for c in sent:
        c.wait_send()


def return_kernel(
    nz,
    nx,
    part,
    info_all,
    stream,
    out,
    from_core,
    for_pair,
    from_pair,
    for_source,
    back,
    mix_high,
    mix_low,
    terms,
    moving,
    landed,
    final,
    core_send,
    core_recv,
    pair_send,
    pair_recv,
    direct_send,
    direct_recv,
    z_send,
    z_recv,
    last_send,
    last_recv,
):
    z, x, h, near = places_around(nz, nx)
    other = 1 - h
    greet(friends(nz, z, h, near))
    tokens, cols = stream.shape
    pairs, per_pair = back.shape[0], back.shape[1]
    mine = pl.multiple_of(h * cols, cols)
    theirs = pl.multiple_of(other * cols, cols)
    sent = []
    arrivals = {}
    order = (4, 3, 2, 1, -3, -2, -1, 0)
    for at, by in enumerate(order):
        source = near(by)
        c = remote(
            part.at[source, :, pl.ds(theirs, cols)],
            from_core.at[source],
            core_send.at[at],
            core_recv.at[at],
            {"hp": other},
        )
        c.start()
        sent.append(c)
        arrivals[by] = c
    slots = pairs * per_pair
    first = (z * slots).astype(F32)
    target = lax.broadcasted_iota(jnp.int32, (slots, 128), 0).astype(F32) + first
    lower = lax.broadcasted_iota(jnp.int32, (8, 128), 1) < tokens
    for j in range(nz // 2):
        both = jnp.where(lower, info_all[2 * j], info_all[2 * j + 1])
        mix = jnp.zeros((slots, 128), F32)
        for k in range(4):
            mix = jnp.where(both[k : k + 1, :] == target, both[4 + k : 5 + k, :], mix)
        high = mix.astype(BF16)
        mix_high[:, 128 * j : 128 * (j + 1)] = high
        mix_low[:, 128 * j : 128 * (j + 1)] = (mix - high.astype(F32)).astype(BF16)

    def whole(by):
        source = near(by)
        arrivals[by].wait_recv()
        return part[source, :, pl.ds(mine, cols)].astype(F32) + from_core[source].astype(F32)

    for k in (3, 2, 1, 0):
        for_pair[k] = whole(1 + k).astype(BF16)
        c = remote(
            for_pair.at[k], from_pair.at[k], pair_send.at[k], pair_recv.at[k], {"ep_1": near(1)}
        )
        c.start()
        sent.append(c)
    pair = x // 2
    for k in (3, 2, 1):
        value = whole(-k)
        remote(
            for_pair.at[k], from_pair.at[k], pair_send.at[k], pair_recv.at[k], {"ep_1": near(1)}
        ).wait_recv()
        for_source[k] = (value + from_pair[k].astype(F32)).astype(BF16)
        c = remote(
            for_source.at[k],
            back.at[pair],
            direct_send.at[k],
            direct_recv.at[k],
            {"ep_1": near(-k)},
        )
        c.start()
        sent.append(c)
    value = whole(0)
    remote(
        for_pair.at[0], from_pair.at[0], pair_send.at[0], pair_recv.at[0], {"ep_1": near(1)}
    ).wait_recv()
    back[pair] = (value + from_pair[0].astype(F32)).astype(BF16)
    for k in ORDER:
        there = back.at[near(REACH[k]) // 2]
        remote(
            there, there, direct_send.at[k], direct_recv.at[k], {"ep_1": near(REACH[k])}
        ).wait_recv()
    results = back[...].reshape(slots, cols)
    over = (((0,), (0,)), ((), ()))
    for j in range(nz // 2):
        at = slice(128 * j, 128 * (j + 1))
        value = lax.dot_general(mix_high[:, at], results, over, preferred_element_type=F32)
        value = value + lax.dot_general(mix_low[:, at], results, over, preferred_element_type=F32)
        terms[2 * j : 2 * j + 2] = value.astype(BF16).reshape(2, tokens, cols)
    half = nz // 2
    subs = 2
    span = tokens // subs
    ways = ((0, shifted(z, 1, nz), half), (1, shifted(z, -1, nz), half - 1))

    def owner(way, step, total):
        return shifted(z, total + 1 - step, nz) if way == 0 else shifted(z, step - total - 1, nz)

    def hop(way, to, step, sub, src):
        at = (way * half + step - 1) * subs + sub
        return remote(
            src,
            landed.at[way, step - 1, pl.ds(sub * span, span), :],
            z_send.at[at],
            z_recv.at[at],
            {"ep_0": to},
        )

    hops = {}
    for step in range(1, half + 1):
        for sub in range(subs):
            at = pl.ds(sub * span, span)
            for way, to, total in ways:
                if step > total:
                    continue
                own = owner(way, step, total)
                if step == 1:
                    c = hop(way, to, step, sub, terms.at[own, at, :])
                else:
                    hops[way, step - 1, sub].wait_recv()
                    moving[way, step - 1, at, :] = (
                        terms[own, at, :].astype(F32) + landed[way, step - 2, at, :].astype(F32)
                    ).astype(BF16)
                    c = hop(way, to, step, sub, moving.at[way, step - 1, at, :])
                c.start()
                sent.append(c)
                hops[way, step, sub] = c
    for sub in range(subs):
        for way, to, total in ways:
            hops[way, total, sub].wait_recv()
    final[...] = (
        stream[...]
        + terms[z].astype(F32)
        + landed[0, half - 1].astype(F32)
        + landed[1, half - 2].astype(F32)
    ).astype(BF16)
    rows = out.shape[0]
    swap = remote(
        final.at[pl.ds(pl.multiple_of(other * rows, rows), rows), :],
        out.at[:, pl.ds(mine, cols)],
        last_send,
        last_recv,
        {"hp": other},
    )
    swap.start()
    out[:, pl.ds(mine, cols)] = final[pl.ds(pl.multiple_of(h * rows, rows), rows), :]
    there = out.at[:, pl.ds(theirs, cols)]
    remote(there, there, last_send, last_recv, {"hp": other}).wait_recv()
    swap.wait_send()
    for c in sent:
        c.wait_send()


def vmem(n):
    return [pl.BlockSpec(memory_space=pltpu.VMEM)] * n


def params(number):
    return pltpu.CompilerParams(collective_id=number, has_side_effects=True)


def picks(blocks, padded, used):
    out = np.zeros((blocks * used, blocks * padded), np.float32)
    for b in range(blocks):
        for i in range(used):
            out[b * used + i, b * padded + i] = 1.0
    return jnp.asarray(out, BF16)


def on_device(
    x_pre,
    x_dec,
    prefill_query_rows,
    prefill_key_values,
    decode_query_rows,
    decode_key_values,
    cache,
    cache_len,
    sinks,
    o_weight,
    norm_gain,
    expert_ids,
    route_logits,
    w_gate_up,
    w_down,
):
    nz, nx = lax.axis_size("ep_0"), lax.axis_size("ep_1")
    dma = pltpu.SemaphoreType.DMA
    width = x_pre.shape[1]
    cols = width // 2
    tokens, topk = expert_ids.shape
    experts = nz * nx // 2
    pairs = nx // 2
    slot = 6
    per_pair = nz * slot
    slots = pairs * per_pair

    earlier = jnp.arange(tokens)[:, None, None, None] < jnp.arange(tokens)[None, None, :, None]
    same = expert_ids[:, :, None, None] == expert_ids[None, None, :, :]
    rank = jnp.sum((earlier & same).astype(jnp.int32), axis=(0, 1))
    z = lax.axis_index("ep_0")
    code = expert_ids // pairs * slots + expert_ids % pairs * per_pair + z * slot + rank
    mix = jax.nn.softmax(route_logits, axis=-1)
    info = jnp.concatenate([code.astype(F32), mix], axis=1).T
    info = jnp.concatenate([info] * (128 // tokens), axis=1)

    attn = attention(
        prefill_query_rows,
        prefill_key_values,
        decode_query_rows,
        decode_key_values,
        cache,
        cache_len,
        sinks,
    )
    attn = jnp.concatenate([attn, jnp.zeros((128 - tokens, attn.shape[1]), BF16)], axis=0)
    heads, per = o_weight.shape
    padded = 16
    weight = jnp.pad(o_weight.T, ((0, padded - per), (0, 0)))
    k_half = heads // 2
    stream, normed, info_all = pl.pallas_call(
        functools.partial(project_kernel, nz, nx, per),
        out_shape=[
            jax.ShapeDtypeStruct((tokens, cols), F32),
            jax.ShapeDtypeStruct((tokens, cols), BF16),
            jax.ShapeDtypeStruct((nz, 8, 128), F32),
        ],
        in_specs=vmem(8),
        out_specs=vmem(3),
        scratch_shapes=[
            pltpu.VMEM((nx, padded, k_half), BF16),
            pltpu.VMEM((nz, padded, k_half), BF16),
            pltpu.VMEM((nz, nx * per, k_half), BF16),
            pltpu.VMEM((nx, nz * per, k_half), BF16),
            pltpu.VMEM((width, 128), F32),
            pltpu.VMEM((width, 128), F32),
            pltpu.VMEM((cols, 128), F32),
            pltpu.VMEM((tokens, 128), F32),
            pltpu.VMEM((tokens, 128), F32),
            ring_sems(nx, 1),
            ring_sems(nx, 1),
            ring_sems(nz, 1),
            ring_sems(nz, 1),
            ring_sems(nz, 2),
            ring_sems(nz, 2),
            ring_sems(nx, 4),
            ring_sems(nx, 4),
            ring_sems(nz, 1),
            ring_sems(nz, 1),
            dma((2,)),
            dma((2,)),
        ],
        compiler_params=params(1),
        name="project",
    )(
        weight,
        attn,
        x_pre,
        x_dec,
        norm_gain.reshape(1, width),
        info,
        picks(nx, padded, per),
        picks(nz, padded, per),
    )
    rows = pl.pallas_call(
        functools.partial(dispatch_kernel, nz, nx),
        out_shape=jax.ShapeDtypeStruct((2, nx, per_pair, cols), BF16),
        in_specs=vmem(2),
        out_specs=vmem(1)[0],
        scratch_shapes=[
            pltpu.VMEM((nz, tokens, cols), BF16),
            pltpu.VMEM((slots, nz * tokens), BF16),
            pltpu.VMEM((pairs, per_pair, cols), BF16),
            ring_sems(nz, 2),
            ring_sems(nz, 2),
            dma((8,)),
            dma((8,)),
            dma((8,)),
            dma((8,)),
            dma((16,)),
            dma((16,)),
        ],
        compiler_params=params(2),
        name="dispatch",
    )(normed, info_all)
    rows = rows.reshape(2, nx * per_pair, cols)

    def into(w):
        return jnp.dot(rows[0], w[:cols], preferred_element_type=F32) + jnp.dot(
            rows[1], w[cols:], preferred_element_type=F32
        )

    gate = into(w_gate_up[0, 0])
    upper = into(w_gate_up[0, 1])
    hidden = ((upper + 1.0) * gate * jax.nn.sigmoid(1.702 * gate)).astype(BF16)
    part = jnp.dot(hidden, w_down[0], preferred_element_type=F32).astype(BF16)
    part = part.reshape(nx, per_pair, width)
    half = nz // 2
    return pl.pallas_call(
        functools.partial(return_kernel, nz, nx),
        out_shape=jax.ShapeDtypeStruct((tokens // 2, width), BF16),
        in_specs=vmem(3),
        out_specs=vmem(1)[0],
        scratch_shapes=[
            pltpu.VMEM((nx, per_pair, cols), BF16),
            pltpu.VMEM((4, per_pair, cols), BF16),
            pltpu.VMEM((4, per_pair, cols), BF16),
            pltpu.VMEM((4, per_pair, cols), BF16),
            pltpu.VMEM((pairs, per_pair, cols), BF16),
            pltpu.VMEM((slots, nz * tokens), BF16),
            pltpu.VMEM((slots, nz * tokens), BF16),
            pltpu.VMEM((nz, tokens, cols), BF16),
            pltpu.VMEM((2, half, tokens, cols), BF16),
            pltpu.VMEM((2, half, tokens, cols), BF16),
            pltpu.VMEM((tokens, cols), BF16),
            dma((8,)),
            dma((8,)),
            dma((4,)),
            dma((4,)),
            dma((4,)),
            dma((4,)),
            ring_sems(nz, 2),
            ring_sems(nz, 2),
            dma,
            dma,
        ],
        compiler_params=params(3),
        name="give_back",
    )(part, info_all, stream)


def solution(mesh):
    torus = Mesh(
        mesh.devices.reshape(mesh.shape["groups"], 16, 8, mesh.shape["hp"]),
        ("groups", "ep_0", "ep_1", "hp"),
    )
    return jax.shard_map(
        on_device,
        mesh=torus,
        in_specs=(
            P(GROUPS_EP, None),
            P(GROUPS_EP, None),
            P(GROUPS_EP, "hp"),
            P(None, GROUPS_EP, "hp"),
            P(GROUPS_EP, "hp"),
            P(None, GROUPS_EP, "hp"),
            P(None, GROUPS_EP, None, "hp"),
            P(GROUPS_EP),
            P("hp"),
            P("hp", EP),
            P(),
            P(GROUPS_EP, None),
            P(GROUPS_EP, None),
            P(EP, None, None, "hp"),
            P(EP, "hp", None),
        ),
        out_specs=P(GROUPS_EP_HP, None),
        check_vma=False,
    )
```

time: 382 us -> 260 us (0.68)
  Pallas kernels: 0 us -> 229 us
  blocking collectives: 186 us -> 0 us
  waiting for transfers between devices: 114 us -> 0 us
  local copies, waits for them, and re-layouts: 36.6 us -> 12.5 us
  between operations: 13.9 us -> 0.21 us
  starting transfers between devices: 12.9 us -> 0 us
    pallas_call x0 -> x3, Pallas kernels: none -> 229 us  [the longest x1 112 us: on_device(): pl.pallas_call(functools.partial(project_kernel, nz, nx, per), out_shape=...]
    all_to_all x5 -> x0, blocking collectives: 121 us -> none  [the longest x1 90.6 us: on_device(): lax.all_to_all(own_plane, EP, split_axis=0, concat_axis=0, tiled=True)]
    all_to_all x1 -> x0, waiting for transfers between devices: 69.4 us -> none  [on_device(): lax.all_to_all(share, EP, split_axis=0, concat_axis=0, tiled=True)]
    all_gather x1 -> x0, blocking collectives: 65.3 us -> none  [all_blocks(): tiles = lax.all_gather(tiles, axes[k], axis=0, tiled=True)]
    all_gather x1 -> x0, waiting for transfers between devices: 44.3 us -> none  [all_blocks(): tiles = lax.all_gather(tiles, axes[k], axis=0, tiled=True)]
    all_to_all x1 -> x0, starting transfers between devices: 12.9 us -> none  [on_device(): lax.all_to_all(share, EP, split_axis=0, concat_axis=0, tiled=True)]
    transpose x3 -> x0, local copies, waits for them, and re-layouts: 11.3 us -> none  [the longest x2 7.43 us: laid_out(): tiles = jnp.moveaxis(tiles, 0, dim)]
    reshape x8 -> x5, local copies, waits for them, and re-layouts: 8.99 us -> 3.5 us  [the longest x1 1.28 us: on_device(): norm_gain.reshape(1, width)]
  transfers between devices with their start and end apart: 2 -> 0, of which waited for: 2 -> 0; matrix products, arithmetic and copies ran while one was open for 2% -> 0% of each run, Pallas kernels for 0% -> 0%
where the time goes in v1:
time: 260 us; the launch traced here: 259 us
  Pallas kernels  229 us (88%)
  local copies, waits for them, and re-layouts  12.5 us (5%)
  matrix products  9.81 us (4%)
  other arithmetic  7.37 us (3%)
    pallas_call x1, Pallas kernels, on_device(): pl.pallas_call(functools.partial(project_kernel, nz, nx, per), out_shape=...  112 us
    pallas_call x1, Pallas kernels, on_device(): pl.pallas_call(functools.partial(return_kernel, nz, nx), out_shape=jax.Sh...  63.9 us
    pallas_call x1, Pallas kernels, on_device(): pl.pallas_call(functools.partial(dispatch_kernel, nz, nx), out_shape=jax....  52.9 us

profile of v1, /device:TPU:65, one launch (start us, length us, event | category | flops | bytes accessed | tf_op | source)
XLA Modules:
  0.0 258.9 jit_solution(15010094008659460644)
XLA Ops:
  0.0 0.8 reduce_max.35
  0.8 0.7 fusion.39
  1.6 0.7 max.32
  2.3 0.7 fusion.38
  3.0 0.7 iota_compare_fusion.2
  3.7 1.3 reshape.126.gain
  5.0 0.7 slice_convert_fusion
  5.9 0.9 convert_reduce_fusion
  6.8 0.7 fusion.34
  7.5 0.7 pad_maximum_fusion.info
  8.2 0.7 fusion.44
  9.1 0.8 reshape.124
  10.1 1.4 pad.4.weight
  11.5 1.1 reshape.122
  12.6 0.4 fusion.46
  13.2 0.3 fusion.7
  13.5 0.2 reshape.123
  13.7 0.5 copy-done.2
  14.5 0.3 fusion.45
  15.2 0.7 copy.93
  16.3 0.3 fusion.9
  16.7 0.8 maximum_maximum_fusion.attn
  17.5 112.2 %project.1 = (f32[64,768]{1,0:T(8,128)}, bf16[64,768]{1,0:T(8,128)(2,1)}, f32[16,8,128]{2,1,0:T(8,128)}) custom-call(bf16[16,1024]{1,0:T(8,128)(2,1)} %pad.4.weight, bf16[128,1024]{1,0:T(8,128)(2,1)} %maximum_maximum_fusion.attn, bf16[56,1536]{1,0:T(8,128)(2,1)} %x_pre.1, bf16[8,1536]{1,0:T(8,128)(2,1)} %x_dec.1, f32[1,1536]{1,0:T(1,128)} %reshape.126.gain, ...), custom_call_target="tpu_custom_call" | custom-call | tf_op jit(solution)/shard_map/project/pallas_call | solution.py:691
  129.7 52.9 %dispatch.1 = bf16[2,8,96,768]{3,2,1,0:T(8,128)(2,1)} custom-call(bf16[64,768]{1,0:T(8,128)(2,1)} %get-tuple-element.8.normed, f32[16,8,128]{2,1,0:T(8,128)} %get-tuple-element.9.info_all), custom_call_target="tpu_custom_call" | custom-call | tf_op jit(solution)/shard_map/dispatch/pallas_call | solution.py:735
  182.6 1.9 fusion.42
  184.5 0.4 copy-done.1
  185.0 0.8 fusion.11
  185.7 0.8 fusion.15
  186.5 1.8 convolution_add_fusion
  188.3 5.1 %convolution_convert_fusion = bf16[768,1536]{1,0:T(8,128)(2,1)} fusion(bf16[1,384,1536]{2,1,0:T(8,128)(2,1)S(1)} %copy-done, f32[768,384]{1,0:T(8,128)} %convolution_add_fusion, f32[768,384]{1,0:T(8,128)S(1)} %fusion.15, bf16[768,768]{1,0:T(8,128)(2,1)S(1)} %bitcast.57, bf16[1,2,1536,384]{3,2,1,0:T(8,128)(2,1)} %param.30), kind=kOutput, calls=%fused_computation | convolution fusion | flops 1362788352 | bytes 7667712 | tf_op jit(solution)/shard_map/dot_general | solution.py:766
  193.4 63.9 %give_back.1 = bf16[32,1536]{1,0:T(8,128)(2,1)} custom-call(bf16[8,96,1536]{2,1,0:T(8,128)(2,1)} %bitcast.58, f32[16,8,128]{2,1,0:T(8,128)} %get-tuple-element.9.info_all, f32[64,768]{1,0:T(8,128)} %get-tuple-element.10.stream), custom_call_target="tpu_custom_call" | custom-call | tf_op jit(solution)/shard_map/give_back/pallas_call | solution.py:769
  257.4 1.5 copy.126
  (32 shorter events, 2.0 us)
Async XLA Ops:
  0.0 188.3 %copy-start = (bf16[1,384,1536]{2,1,0:T(8,128)(2,1)S(1)}, bf16[1,384,1536]{2,1,0:T(8,128)(2,1)}, u32[]{:S(2)}) copy-start(bf16[1,384,1536]{2,1,0:T(8,128)(2,1)} %param.31) | copy-start | bytes 3538948
  13.2 1.0 copy-start.2
  182.6 2.4 copy-start.1

commit v2 on v1

v2 whole, which is shorter than its diff:
```python
import functools

import jax
import jax.numpy as jnp
import numpy as np
from jax import lax
from jax.experimental import pallas as pl
from jax.experimental.pallas import tpu as pltpu
from jax.sharding import Mesh
from jax.sharding import PartitionSpec as P

HEAD_SIZE = 64
EP = ("ep_0", "ep_1")
GROUPS_EP = ("groups", "ep_0", "ep_1")
GROUPS_EP_HP = ("groups", "ep_0", "ep_1", "hp")
EPS = 1e-05
SLOT = 6
MESH = pl.DeviceIdType.MESH
F32 = jnp.float32
BF16 = jnp.bfloat16


def remote(src, dst, send_sem, recv_sem, where):
    return pltpu.make_async_remote_copy(
        src_ref=src,
        dst_ref=dst,
        send_sem=send_sem,
        recv_sem=recv_sem,
        device_id=where,
        device_id_type=MESH,
    )


def greet(places):
    barrier = pltpu.get_barrier_semaphore()
    for place in places:
        pl.semaphore_signal(barrier, inc=1, device_id=place, device_id_type=MESH)
    pl.semaphore_wait(barrier, len(places))


def shifted(me, by, n):
    return lax.rem(me + (by + 2 * n), n)


def ring_gather(axis, n, me, view, subs, send_sems, recv_sems, sent):
    half = n // 2
    ways = ((0, -1, shifted(me, 1, n)), (1, 1, shifted(me, -1, n)))

    def used(step, way, sub):
        return step < half or sub % 2 == way

    def copy(step, way, sign, to, sub):
        block = view(shifted(me, sign * (step - 1), n), sub)
        at = (way * half + step - 1) * subs + sub
        return remote(block, block, send_sems.at[at], recv_sems.at[at], {axis: to})

    def arrival(step, way, sign, to, sub):
        block = view(shifted(me, sign * step, n), sub)
        at = (way * half + step - 1) * subs + sub
        return remote(block, block, send_sems.at[at], recv_sems.at[at], {axis: to})

    for sub in range(subs):
        for way, sign, to in ways:
            if used(1, way, sub):
                c = copy(1, way, sign, to, sub)
                c.start()
                sent.append(c)
    yield
    for step in range(1, half + 1):
        for sub in range(subs):
            for way, sign, to in ways:
                if not used(step, way, sub):
                    continue
                arrival(step, way, sign, to, sub).wait_recv()
                if step < half and used(step + 1, way, sub):
                    c = copy(step + 1, way, sign, to, sub)
                    c.start()
                    sent.append(c)
        yield


def place_of(way, step, n):
    if step == 0:
        return 0
    if step == n // 2:
        return n - 1
    return 2 * step - 1 + way


def ring_gather_near(axis, n, me, view, subs, send_sems, recv_sems, sent):
    half = n // 2
    ways = ((0, shifted(me, 1, n)), (1, shifted(me, -1, n)))

    def used(step, way, sub):
        return step < half or sub % 2 == way

    def copy(step, way, to, sub):
        at = (way * half + step - 1) * subs + sub
        return remote(
            view(place_of(way, step - 1, n), sub),
            view(place_of(way, step, n), sub),
            send_sems.at[at],
            recv_sems.at[at],
            {axis: to},
        )

    flights = {}

    def launch(step, way, to, sub):
        c = copy(step, way, to, sub)
        c.start()
        sent.append(c)
        flights[step, way, sub] = c

    for sub in range(subs):
        for way, to in ways:
            if used(1, way, sub):
                launch(1, way, to, sub)
    yield
    for step in range(1, half + 1):
        for sub in range(subs):
            for way, to in ways:
                if not used(step, way, sub):
                    continue
                flights[step, way, sub].wait_recv()
                if step < half and used(step + 1, way, sub):
                    launch(step + 1, way, to, sub)
        yield


def ring_sems(n, subs):
    return pltpu.SemaphoreType.DMA((n * subs,))


def nt(a, b):
    return lax.dot_general(a, b, (((1,), (1,)), ((), ())), preferred_element_type=F32)


def iota(shape, dim):
    return lax.broadcasted_iota(jnp.int32, shape, dim)


def probability(scores, sink):
    top = jnp.maximum(jnp.max(scores, axis=-1, keepdims=True), sink)
    expo = jnp.exp(scores - top)
    total = jnp.sum(expo, axis=-1, keepdims=True) + jnp.exp(sink - top)
    return expo, total, top


def attention(pq, pkv, dq, dkv, cache, cache_len, sinks, attn):
    n_pre, n_dec = pq.shape[0], dq.shape[0]
    kv_heads = pkv.shape[2] // HEAD_SIZE
    q_heads = pq.shape[1] // HEAD_SIZE
    group = q_heads // kv_heads
    kv_max = cache.shape[2]
    scale = HEAD_SIZE ** (-0.5)
    visible = iota((n_pre, n_pre), 1) <= iota((n_pre, n_pre), 0)
    attn[n_pre + n_dec :, :] = jnp.zeros((attn.shape[0] - n_pre - n_dec, attn.shape[1]), F32)
    for g in range(q_heads):
        at = slice(g * HEAD_SIZE, (g + 1) * HEAD_SIZE)
        j = g // group
        kv = slice(j * HEAD_SIZE, (j + 1) * HEAD_SIZE)
        scores = nt(pq[:, at], pkv[0, :, kv]) * scale
        scores = jnp.where(visible, scores, -jnp.inf)
        expo, total, _ = probability(scores, sinks[:, g : g + 1])
        weight = (expo / total).astype(BF16)
        value = jnp.dot(weight, pkv[1, :, kv], preferred_element_type=F32)
        attn[0:n_pre, at] = value.astype(BF16).astype(F32)
        if g % 2 == 1:
            yield
    rows = group * n_dec
    which = lax.rem(iota((rows, kv_max), 0), n_dec)
    live = iota((n_dec, kv_max), 1) < cache_len[...]
    live = jnp.concatenate([live.astype(F32)] * group, axis=0) > 0.5
    every = dq[...].astype(F32)
    for j in range(kv_heads):
        kv = slice(j * HEAD_SIZE, (j + 1) * HEAD_SIZE)
        heads = range(j * group, (j + 1) * group)
        queries = jnp.concatenate(
            [every[:, g * HEAD_SIZE : (g + 1) * HEAD_SIZE] for g in heads], axis=0
        )
        narrow = queries.astype(BF16)
        scores = jnp.zeros((rows, kv_max), F32)
        for s in range(n_dec):
            scores = jnp.where(which == s, nt(narrow, cache[0, s, :, kv]), scores)
        scores = jnp.where(live, scores * scale, -jnp.inf)
        own_key = jnp.concatenate([dkv[0, :, kv].astype(F32)] * group, axis=0)
        own_value = jnp.concatenate([dkv[1, :, kv].astype(F32)] * group, axis=0)
        own = jnp.sum(queries * own_key, axis=-1, keepdims=True) * scale
        sink = jnp.concatenate(
            [jnp.broadcast_to(sinks[:, g : g + 1], (n_dec, 1)) for g in heads], axis=0
        )
        top = jnp.maximum(jnp.maximum(jnp.max(scores, axis=-1, keepdims=True), own), sink)
        expo = jnp.exp(scores - top)
        own = jnp.exp(own - top)
        total = jnp.sum(expo, axis=-1, keepdims=True) + own + jnp.exp(sink - top)
        weight = expo / total
        yield
        value = (own / total).astype(BF16).astype(F32) * own_value
        for s in range(n_dec):
            value = value + jnp.dot(
                jnp.where(which == s, weight, 0.0).astype(BF16),
                cache[1, s, :, kv],
                preferred_element_type=F32,
            )
        value = value.astype(BF16).astype(F32)
        for i, g in enumerate(heads):
            attn[n_pre : n_pre + n_dec, g * HEAD_SIZE : (g + 1) * HEAD_SIZE] = value[
                i * n_dec : (i + 1) * n_dec
            ]
        yield


def routes(nz, nx, groups, z, expert_ids, route_logits):
    tokens, topk = expert_ids.shape
    pairs = nx // 2
    near = nz // groups
    ids = expert_ids[...].astype(F32)
    lane = iota((tokens, 128), 1).astype(F32)
    named = jnp.zeros((tokens, 128), F32)
    for k in range(topk):
        named = jnp.where(lane == ids[:, k : k + 1], 1.0, named)
    before = (iota((tokens, tokens), 1) < iota((tokens, tokens), 0)).astype(F32).astype(BF16)
    count = jnp.dot(before, named.astype(BF16), preferred_element_type=F32)
    logits = route_logits[...]
    expo = jnp.exp(logits - jnp.max(logits, axis=-1, keepdims=True))
    mix = expo / jnp.sum(expo, axis=-1, keepdims=True)
    there = jnp.floor(ids * (1.0 / pairs))
    pair = ids - there * pairs
    ahead = z.astype(F32) - there
    ahead = jnp.where(ahead < 0.0, ahead + nz, ahead)
    half = nz // 2
    spot = jnp.where(
        ahead < half, 2.0 * ahead, jnp.where(ahead == half, nz - 1.0, 2.0 * nz - 1.0 - 2.0 * ahead)
    )
    group = jnp.floor(spot * (1.0 / near))
    code = ((there * groups + group) * pairs + pair) * (near * SLOT) + (spot - group * near) * SLOT
    table = jnp.zeros((tokens, 128), F32)
    for k in range(topk):
        rank = jnp.sum(jnp.where(lane == ids[:, k : k + 1], count, 0.0), axis=-1, keepdims=True)
        table = jnp.where(lane == k, code[:, k : k + 1] + rank, table)
        table = jnp.where(lane == 4 + k, mix[:, k : k + 1], table)
    table = jnp.concatenate([table] * (128 // tokens), axis=0)
    return jnp.transpose(table)[0:8]


def project_kernel(
    nz,
    nx,
    groups,
    k_a,
    weight,
    pq,
    pkv,
    dq,
    dkv,
    cache,
    cache_len,
    sinks,
    x_pre,
    x_dec,
    gain,
    expert_ids,
    route_logits,
    pick_a,
    pick_b,
    stream,
    normed,
    info_all,
    attn,
    small_a,
    small_b,
    big_a,
    big_b,
    sum_a,
    sum_b,
    from_core,
    squares,
    squares_in,
    small_a_send,
    small_a_recv,
    small_b_send,
    small_b_recv,
    big_a_send,
    big_a_recv,
    big_b_send,
    big_b_recv,
    info_send,
    info_recv,
    core_send,
    core_recv,
):
    z, x, h = lax.axis_index("ep_0"), lax.axis_index("ep_1"), lax.axis_index("hp")
    other = 1 - h
    greet(
        [
            {"ep_0": shifted(z, 1, nz)},
            {"ep_0": shifted(z, -1, nz)},
            {"ep_1": shifted(x, 1, nx)},
            {"ep_1": shifted(x, -1, nx)},
            {"hp": other},
        ]
    )
    heads, w = weight.shape
    tokens, cols = stream.shape
    padded = small_a.shape[1]
    eye = (iota((padded, w), 0) == iota((padded, w), 1)).astype(F32).astype(BF16)
    turned = nt(eye, weight[...]).astype(BF16)
    small_a[x] = turned[:, 0:k_a]
    small_b[z] = turned[:, k_a:heads]
    sent = []
    ring_a = ring_gather(
        "ep_1", nx, x, lambda b, s: small_a.at[b], 1, small_a_send, small_a_recv, sent
    )
    ring_b = ring_gather(
        "ep_0", nz, z, lambda b, s: small_b.at[b], 1, small_b_send, small_b_recv, sent
    )
    next(ring_a)
    next(ring_b)
    info_all[0] = routes(nz, nx, groups, z, expert_ids, route_logits)
    tell = ring_gather_near(
        "ep_0", nz, z, lambda b, s: info_all.at[b], 1, info_send, info_recv, sent
    )
    next(tell)
    work = attention(pq, pkv, dq, dkv, cache, cache_len, sinks, attn)
    a_rows = big_a.shape[1]
    b_rows = big_b.shape[1]
    for _ in range(nx // 2):
        next(work, None)
        next(ring_a)
        next(ring_b)
    packed = jnp.dot(pick_a[...], small_a[...].reshape(nx * padded, k_a), preferred_element_type=F32)
    big_a[z] = packed.astype(BF16)
    large_a = ring_gather(
        "ep_0",
        nz,
        z,
        lambda b, s: big_a.at[b, pl.ds(s * (a_rows // 2), a_rows // 2), :],
        2,
        big_a_send,
        big_a_recv,
        sent,
    )
    next(large_a)
    for _ in range(nz // 2 - nx // 2):
        next(ring_b)
        next(work, None)
        next(large_a)
        next(tell)
    packed = jnp.dot(
        pick_b[...], small_b[...].reshape(nz * padded, heads - k_a), preferred_element_type=F32
    )
    big_b[x] = packed.astype(BF16)
    large_b = ring_gather(
        "ep_1",
        nx,
        x,
        lambda b, s: big_b.at[b, pl.ds(s * (b_rows // 4), b_rows // 4), :],
        4,
        big_b_send,
        big_b_recv,
        sent,
    )
    next(large_b)
    for _ in range(nx // 2):
        next(large_a)
        next(work, None)
        next(work, None)
        next(tell)
        next(large_b)
    for _ in work:
        pass
    attn_a = attn[:, 0:k_a].astype(BF16)
    attn_b = attn[:, k_a:heads].astype(BF16)
    for b in range(nz):
        sum_a[b * a_rows : (b + 1) * a_rows, :] = nt(big_a[b], attn_a)
    for b in range(nx):
        sum_b[b * b_rows : (b + 1) * b_rows, :] = nt(big_b[b], attn_b)
    for b in range(nz):
        for c in range(nx):
            at_a = (b * nx + c) * w
            at_b = (c * nz + b) * w
            sum_a[at_a : at_a + w, :] = sum_a[at_a : at_a + w, :] + sum_b[at_b : at_b + w, :]
    mine = pl.multiple_of(h * cols, cols)
    theirs = pl.multiple_of(other * cols, cols)
    swap = remote(
        sum_a.at[pl.ds(theirs, cols), :],
        from_core,
        core_send.at[0],
        core_recv.at[0],
        {"hp": other},
    )
    swap.start()
    swap.wait()
    summed = jnp.transpose(sum_a[pl.ds(mine, cols), :] + from_core[...])
    n_pre = x_pre.shape[0]
    stream[0:n_pre, :] = summed[0:n_pre] + x_pre[:, pl.ds(mine, cols)].astype(F32)
    stream[n_pre:tokens, :] = summed[n_pre:tokens] + x_dec[:, pl.ds(mine, cols)].astype(F32)
    value = stream[...]
    total = jnp.sum(value * value, axis=-1, keepdims=True)
    squares[...] = jnp.broadcast_to(total, squares.shape)
    swap = remote(squares, squares_in, core_send.at[1], core_recv.at[1], {"hp": other})
    swap.start()
    swap.wait()
    total = total + squares_in[:, 0:1]
    scale = lax.rsqrt(total / (2 * cols) + EPS)
    normed[...] = (value * scale * gain[:, pl.ds(mine, cols)]).astype(BF16)
    for c in sent:
        c.wait_send()


def places_around(nz, nx):
    z, x, h = lax.axis_index("ep_0"), lax.axis_index("ep_1"), lax.axis_index("hp")
    sign = 1 - 2 * lax.rem(x, 2)

    def near(by):
        return lax.rem(x + by * sign + 2 * nx, nx)

    return z, x, h, near


REACH = {1: -1, 2: 2, 3: -3}
ORDER = (3, 2, 1)


def friends(nz, z, h, near):
    return [
        {"ep_0": shifted(z, 1, nz)},
        {"ep_0": shifted(z, -1, nz)},
        {"hp": 1 - h},
        {"ep_1": near(1)},
        {"ep_1": near(-1)},
        {"ep_1": near(2)},
        {"ep_1": near(-2)},
        {"ep_1": near(-3)},
    ]


def experts_kernel(
    nz,
    nx,
    groups,
    normed,
    info_all,
    stream,
    w_in,
    w_out,
    out,
    gate_up,
    down,
    tok,
    onehot,
    mix_high,
    mix_low,
    picked,
    rows,
    part,
    from_core,
    for_pair,
    from_pair,
    for_source,
    back,
    terms,
    moving,
    landed,
    final,
    load_sem,
    z_send,
    z_recv,
    direct_send,
    direct_recv,
    pair_send,
    pair_recv,
    core_send,
    core_recv,
    sums_send,
    sums_recv,
    up_send,
    up_recv,
    home_send,
    home_recv,
    add_send,
    add_recv,
    last_send,
    last_recv,
):
    z, x, h, near = places_around(nz, nx)
    other = 1 - h
    loads = [
        pltpu.make_async_copy(w_in.at[0], gate_up, load_sem.at[0]),
        pltpu.make_async_copy(w_out.at[0], down, load_sem.at[1]),
    ]
    for c in loads:
        c.start()
    greet(friends(nz, z, h, near))
    tokens, cols = normed.shape
    pairs = nx // 2
    spots = nz // groups
    per = spots * SLOT
    block = pairs * per
    mine = x // 2
    sent = []
    tok[0] = normed[...]
    span = tokens // 2
    ring = ring_gather_near(
        "ep_0", nz, z, lambda b, s: tok.at[b, pl.ds(s * span, span), :], 2, z_send, z_recv, sent
    )
    next(ring)
    lower = iota((8, 128), 1) < tokens
    for g in range(groups):
        first = ((z * groups + g) * block).astype(F32)
        target = iota((block, 128), 0).astype(F32) + first
        for i in range(spots // 2):
            j = g * spots + 2 * i
            both = jnp.where(lower, info_all[j], info_all[j + 1])
            hit = jnp.zeros((block, 128), F32)
            mix = jnp.zeros((block, 128), F32)
            for k in range(4):
                same = both[k : k + 1, :] == target
                hit = jnp.where(same, 1.0, hit)
                mix = jnp.where(same, both[4 + k : 5 + k, :], mix)
            at = slice(128 * i, 128 * (i + 1))
            onehot[g, :, at] = hit.astype(BF16)
            high = mix.astype(BF16)
            mix_high[g, :, at] = high
            mix_low[g, :, at] = (mix - high.astype(F32)).astype(BF16)

    def start(c):
        c.start()
        sent.append(c)
        return c

    crossings = {}

    def cross(g, source, at):
        here, there = rows.at[h, g, source], rows.at[other, g, source]
        sems = core_send.at[8 * g + at], core_recv.at[8 * g + at]
        start(remote(here, here, *sems, {"hp": other}))
        crossings[g, at] = remote(there, there, *sems, {"hp": other})

    def dispatch(g):
        blocks = tok[g * spots : (g + 1) * spots].reshape(spots * tokens, cols)
        chosen = jnp.dot(onehot[g], blocks, preferred_element_type=F32).astype(BF16)
        picked[g] = chosen.reshape(pairs, per, cols)
        for k in ORDER:
            to = near(REACH[k])
            start(
                remote(
                    picked.at[g, to // 2],
                    rows.at[h, g, x],
                    direct_send.at[4 * g + k],
                    direct_recv.at[4 * g + k],
                    {"ep_1": to},
                )
            )
        start(
            remote(
                picked.at[g, mine],
                rows.at[h, g, x],
                pair_send.at[4 * g],
                pair_recv.at[4 * g],
                {"ep_1": near(1)},
            )
        )
        rows[h, g, x] = picked[g, mine]
        cross(g, x, 0)

    def pass_on(g):
        for k in (1, 2, 3):
            source = near(-k)
            at = 4 * g + k
            here = rows.at[h, g, source]
            to = {"ep_1": near(1)}
            remote(here, here, direct_send.at[at], direct_recv.at[at], to).wait_recv()
            start(remote(here, here, pair_send.at[at], pair_recv.at[at], to))
            cross(g, source, k)

    def collect(g):
        for k in range(4):
            source = near(1 + k)
            at = 4 * g + k
            here = rows.at[h, g, source]
            to = {"ep_1": near(1)}
            remote(here, here, pair_send.at[at], pair_recv.at[at], to).wait_recv()
            cross(g, source, 4 + k)

    partials = {}

    def feed(g):
        for at in range(8):
            crossings[g, at].wait_recv()
        left = rows[0, g].reshape(nx * per, cols)
        right = rows[1, g].reshape(nx * per, cols)

        def into(i):
            return jnp.dot(left, gate_up[i, 0:cols, :], preferred_element_type=F32) + jnp.dot(
                right, gate_up[i, cols : 2 * cols, :], preferred_element_type=F32
            )

        gate = into(0)
        upper = into(1)
        hidden = ((upper + 1.0) * gate * jax.nn.sigmoid(1.702 * gate)).astype(BF16)
        for i in range(2):
            value = jnp.dot(hidden, down[:, i * cols : (i + 1) * cols], preferred_element_type=F32)
            part[i, g] = value.astype(BF16).reshape(nx, per, cols)
        partials[g] = start(
            remote(
                part.at[other, g], from_core.at[g], sums_send.at[g], sums_recv.at[g], {"hp": other}
            )
        )

    def whole(g, by):
        source = near(by)
        return part[h, g, source].astype(F32) + from_core[g, source].astype(F32)

    def give(g):
        partials[g].wait_recv()
        for k in (3, 2, 1, 0):
            for_pair[g, k] = whole(g, 1 + k).astype(BF16)
            at = 4 * g + k
            start(
                remote(
                    for_pair.at[g, k],
                    from_pair.at[g, k],
                    up_send.at[at],
                    up_recv.at[at],
                    {"ep_1": near(1)},
                )
            )

    def take(g, k):
        at = 4 * g + k
        remote(
            for_pair.at[g, k],
            from_pair.at[g, k],
            up_send.at[at],
            up_recv.at[at],
            {"ep_1": near(1)},
        ).wait_recv()
        return (whole(g, -k) + from_pair[g, k].astype(F32)).astype(BF16)

    def send_home(g):
        for k in (3, 2, 1):
            for_source[g, k] = take(g, k)
            start(
                remote(
                    for_source.at[g, k],
                    back.at[g, mine],
                    home_send.at[4 * g + k],
                    home_recv.at[4 * g + k],
                    {"ep_1": near(-k)},
                )
            )
        back[g, mine] = take(g, 0)

    over = (((0,), (0,)), ((), ()))

    def combine(g):
        for k in ORDER:
            to = near(REACH[k])
            there = back.at[g, to // 2]
            at = 4 * g + k
            remote(there, there, home_send.at[at], home_recv.at[at], {"ep_1": to}).wait_recv()
        results = back[g].reshape(block, cols)
        value = lax.dot_general(mix_high[g], results, over, preferred_element_type=F32)
        value = value + lax.dot_general(mix_low[g], results, over, preferred_element_type=F32)
        terms[g * spots : (g + 1) * spots] = value.astype(BF16).reshape(spots, tokens, cols)

    half = nz // 2
    ways = ((0, shifted(z, 1, nz)), (1, shifted(z, -1, nz)))
    hops = {}

    def reduce_step(step):
        for sub in range(2):
            at = pl.ds(sub * span, span)
            for way, to in ways:
                if step == 1 and sub != way:
                    continue
                distance = half + 1 - step
                spot = place_of(1 - way, distance, nz)
                if step == 1 or (step == 2 and sub != way):
                    src = terms.at[spot, at, :]
                else:
                    hops[way, step - 1, sub].wait_recv()
                    moving[way, step - 1, at, :] = (
                        terms[spot, at, :].astype(F32) + landed[way, step - 2, at, :].astype(F32)
                    ).astype(BF16)
                    src = moving.at[way, step - 1, at, :]
                n = (way * half + step - 1) * 2 + sub
                hops[way, step, sub] = start(
                    remote(
                        src,
                        landed.at[way, step - 1, at, :],
                        add_send.at[n],
                        add_recv.at[n],
                        {"ep_0": to},
                    )
                )

    def reduce_from(g):
        for step in range(1, half + 1):
            if step not in done and (half + 1 - step) * 2 - 1 >= g * spots:
                done.add(step)
                reduce_step(step)

    done = set()
    pace = spots // 2
    last = groups - 1
    for step in range(1, half + 1):
        next(ring)
        g, phase = divmod(step, pace)
        if phase == 0:
            dispatch(g - 1)
        elif phase == pace // 2 and g >= 2:
            pass_on(g - 2)
    for c in loads:
        c.wait()
    for g in range(max(0, groups - 2), groups - 1):
        pass_on(g)
    for g in range(groups):
        if g == last - 1:
            pass_on(last)
        collect(g)
        if g == last:
            give(last - 1)
        feed(g)
    give(last)
    for g in range(last, -1, -1):
        send_home(g)
        if g >= 2:
            give(g - 2)
        if g < last:
            combine(g + 1)
            reduce_from(g + 1)
    combine(0)
    reduce_from(0)
    for sub in range(2):
        for way, _ in ways:
            hops[way, half, sub].wait_recv()
    final[...] = (
        stream[...]
        + terms[0].astype(F32)
        + landed[0, half - 1].astype(F32)
        + landed[1, half - 1].astype(F32)
    ).astype(BF16)
    count = out.shape[0]
    left = pl.multiple_of(h * cols, cols)
    right = pl.multiple_of(other * cols, cols)
    swap = remote(
        final.at[pl.ds(pl.multiple_of(other * count, count), count), :],
        out.at[:, pl.ds(left, cols)],
        last_send,
        last_recv,
        {"hp": other},
    )
    swap.start()
    out[:, pl.ds(left, cols)] = final[pl.ds(pl.multiple_of(h * count, count), count), :]
    there = out.at[:, pl.ds(right, cols)]
    remote(there, there, last_send, last_recv, {"hp": other}).wait_recv()
    swap.wait_send()
    for c in sent:
        c.wait_send()


def vmem(n):
    return [pl.BlockSpec(memory_space=pltpu.VMEM)] * n


def params(number):
    return pltpu.CompilerParams(collective_id=number, has_side_effects=True)


def picks(blocks, padded, used):
    out = np.zeros((blocks * used, blocks * padded), np.float32)
    for b in range(blocks):
        for i in range(used):
            out[b * used + i, b * padded + i] = 1.0
    return jnp.asarray(out, BF16)


def on_device(
    x_pre,
    x_dec,
    prefill_query_rows,
    prefill_key_values,
    decode_query_rows,
    decode_key_values,
    cache,
    cache_len,
    sinks,
    o_weight,
    norm_gain,
    expert_ids,
    route_logits,
    w_gate_up,
    w_down,
):
    nz, nx = lax.axis_size("ep_0"), lax.axis_size("ep_1")
    dma = pltpu.SemaphoreType.DMA
    width = x_pre.shape[1]
    cols = width // 2
    tokens = expert_ids.shape[0]
    pairs = nx // 2
    groups = 4
    heads, w = o_weight.shape
    padded = 16
    k_a = heads * 5 // 8
    stream, normed, info_all = pl.pallas_call(
        functools.partial(project_kernel, nz, nx, groups, k_a),
        out_shape=[
            jax.ShapeDtypeStruct((tokens, cols), F32),
            jax.ShapeDtypeStruct((tokens, cols), BF16),
            jax.ShapeDtypeStruct((nz, 8, 128), F32),
        ],
        in_specs=vmem(15),
        out_specs=vmem(3),
        scratch_shapes=[
            pltpu.VMEM((128, heads), F32),
            pltpu.VMEM((nx, padded, k_a), BF16),
            pltpu.VMEM((nz, padded, heads - k_a), BF16),
            pltpu.VMEM((nz, nx * w, k_a), BF16),
            pltpu.VMEM((nx, nz * w, heads - k_a), BF16),
            pltpu.VMEM((width, 128), F32),
            pltpu.VMEM((width, 128), F32),
            pltpu.VMEM((cols, 128), F32),
            pltpu.VMEM((tokens, 128), F32),
            pltpu.VMEM((tokens, 128), F32),
            ring_sems(nx, 1),
            ring_sems(nx, 1),
            ring_sems(nz, 1),
            ring_sems(nz, 1),
            ring_sems(nz, 2),
            ring_sems(nz, 2),
            ring_sems(nx, 4),
            ring_sems(nx, 4),
            ring_sems(nz, 1),
            ring_sems(nz, 1),
            dma((2,)),
            dma((2,)),
        ],
        compiler_params=params(1),
        name="project",
    )(
        o_weight,
        prefill_query_rows,
        prefill_key_values,
        decode_query_rows,
        decode_key_values,
        cache,
        cache_len.reshape(-1, 1),
        sinks.reshape(1, -1),
        x_pre,
        x_dec,
        norm_gain.reshape(1, width),
        expert_ids,
        route_logits,
        picks(nx, padded, w),
        picks(nz, padded, w),
    )
    half = nz // 2
    spots = nz // groups
    per = spots * SLOT
    block = pairs * per
    anywhere = pl.BlockSpec(memory_space=pl.ANY)
    return pl.pallas_call(
        functools.partial(experts_kernel, nz, nx, groups),
        out_shape=jax.ShapeDtypeStruct((tokens // 2, width), BF16),
        in_specs=vmem(3) + [anywhere, anywhere],
        out_specs=vmem(1)[0],
        scratch_shapes=[
            pltpu.VMEM(w_gate_up.shape[1:], BF16),
            pltpu.VMEM(w_down.shape[1:], BF16),
            pltpu.VMEM((nz, tokens, cols), BF16),
            pltpu.VMEM((groups, block, spots * tokens), BF16),
            pltpu.VMEM((groups, block, spots * tokens), BF16),
            pltpu.VMEM((groups, block, spots * tokens), BF16),
            pltpu.VMEM((groups, pairs, per, cols), BF16),
            pltpu.VMEM((2, groups, nx, per, cols), BF16),
            pltpu.VMEM((2, groups, nx, per, cols), BF16),
            pltpu.VMEM((groups, nx, per, cols), BF16),
            pltpu.VMEM((groups, 4, per, cols), BF16),
            pltpu.VMEM((groups, 4, per, cols), BF16),
            pltpu.VMEM((groups, 4, per, cols), BF16),
            pltpu.VMEM((groups, pairs, per, cols), BF16),
            pltpu.VMEM((nz, tokens, cols), BF16),
            pltpu.VMEM((2, half, tokens, cols), BF16),
            pltpu.VMEM((2, half, tokens, cols), BF16),
            pltpu.VMEM((tokens, cols), BF16),
            dma((2,)),
            ring_sems(nz, 2),
            ring_sems(nz, 2),
            dma((groups * 4,)),
            dma((groups * 4,)),
            dma((groups * 4,)),
            dma((groups * 4,)),
            dma((groups * 8,)),
            dma((groups * 8,)),
            dma((groups,)),
            dma((groups,)),
            dma((groups * 4,)),
            dma((groups * 4,)),
            dma((groups * 4,)),
            dma((groups * 4,)),
            ring_sems(nz, 2),
            ring_sems(nz, 2),
            dma,
            dma,
        ],
        compiler_params=params(2),
        name="layer",
    )(normed, info_all, stream, w_gate_up, w_down)


def solution(mesh):
    torus = Mesh(
        mesh.devices.reshape(mesh.shape["groups"], 16, 8, mesh.shape["hp"]),
        ("groups", "ep_0", "ep_1", "hp"),
    )
    return jax.shard_map(
        on_device,
        mesh=torus,
        in_specs=(
            P(GROUPS_EP, None),
            P(GROUPS_EP, None),
            P(GROUPS_EP, "hp"),
            P(None, GROUPS_EP, "hp"),
            P(GROUPS_EP, "hp"),
            P(None, GROUPS_EP, "hp"),
            P(None, GROUPS_EP, None, "hp"),
            P(GROUPS_EP),
            P("hp"),
            P("hp", EP),
            P(),
            P(GROUPS_EP, None),
            P(GROUPS_EP, None),
            P(EP, None, None, "hp"),
            P(EP, "hp", None),
        ),
        out_specs=P(GROUPS_EP_HP, None),
        check_vma=False,
    )
```

time: 260 us -> 201 us (0.77)
  Pallas kernels: 229 us -> 192 us
  matrix products: 9.81 us -> 0 us
  other arithmetic: 7.37 us -> 0 us
  local copies, waits for them, and re-layouts: 12.5 us -> 8.52 us
    pallas_call x3 -> x2, Pallas kernels: 229 us -> 192 us  [the longest x1 100 us: on_device(): pl.pallas_call(functools.partial(project_kernel, nz, nx, groups, k_a), ou...]
    dot_general x9 -> x0, matrix products: 9.81 us -> none  [the longest x1 5.12 us: on_device(): part = jnp.dot(hidden, w_down[0], preferred_element_type=F32).astype(BF16)]
    unnamed x7 -> x4, local copies, waits for them, and re-layouts: 2.52 us -> 5.92 us
    slice x6 -> x0, local copies, waits for them, and re-layouts: 3.09 us -> none  [the longest x1 1.93 us: into(): rows[1]]
where the time goes in v2:
time: 201 us
  Pallas kernels  192 us (96%)
  local copies, waits for them, and re-layouts  8.52 us (4%)
    pallas_call x1, Pallas kernels, on_device(): pl.pallas_call(functools.partial(project_kernel, nz, nx, groups, k_a), ou...  100 us
    pallas_call x1, Pallas kernels, on_device(): pl.pallas_call(functools.partial(experts_kernel, nz, nx, groups), out_sha...  91.7 us
    unnamed x4, local copies, waits for them, and re-layouts  5.92 us

profile of v2, /device:TPU:65, one launch (start us, length us, event | category | flops | bytes accessed | tf_op | source)
XLA Modules:
  0.0 200.6 jit_solution(3013770020152173931)
XLA Ops:
  0.0 1.3 copy.19.cache_len
  1.3 1.3 reshape.11.gain
  2.6 1.4 copy.20.expert_ids
  4.0 1.4 copy.21.route_logits
  5.4 1.6 copy.18.weight
  7.0 100.3 %project.1 = (f32[64,768]{1,0:T(8,128)}, bf16[64,768]{1,0:T(8,128)(2,1)}, f32[16,8,128]{2,1,0:T(8,128)}) custom-call(bf16[1024,12]{1,0:T(8,128)(2,1)} %copy.18.weight, bf16[56,1024]{1,0:T(8,128)(2,1)} %pq.1, bf16[2,56,128]{2,1,0:T(8,128)(2,1)} %pkv.1, bf16[8,1024]{1,0:T(8,128)(2,1)} %dq.1, bf16[2,8,128]{2,1,0:T(8,128)(2,1)} %dkv.1, ...), custom_call_target="tpu_custom_call" | custom-call | tf_op jit(solution)/shard_map/project/pallas_call | solution.py:808
  107.3 91.7 %layer.1 = bf16[32,1536]{1,0:T(8,128)(2,1)} custom-call(bf16[64,768]{1,0:T(8,128)(2,1)} %get-tuple-element.8.normed, f32[16,8,128]{2,1,0:T(8,128)} %get-tuple-element.9.info_all, f32[64,768]{1,0:T(8,128)} %get-tuple-element.10.stream, bf16[1,2,1536,384]{3,2,1,0:T(8,128)(2,1)} %w_in.1, bf16[1,384,1536]{2,1,0:T(8,128)(2,1)} %w_out.1), custom_call_target="tpu_custom_call" | custom-call | tf_op jit(solution)/shard_map/layer/pallas_call | solution.py:865
  199.0 1.5 copy.23
